TPU v7x, 32 devices: a whole 2x2x4 slice. The times are simulated.
32 devices in a mesh: row: 8 (over z, x), col: 4 (over y, core).
Axes of the slice: x: 2, y: 2, z: 4, core: 2. Of those that a mesh axis runs over, the one named last changes fastest.
Arguments:
- source_points: bfloat16 [512, 64, 128], P(('row', 'col')), may hold values from -1.5 to 1.5
- target_points: bfloat16 [512, 64, 128], P(('row', 'col')), may hold values from -1.5 to 1.5
- source_mass: float32 [512, 128], P(('row', 'col')), may hold values from -4 to 4
- target_mass: float32 [512, 128], P(('row', 'col')), may hold values from -4 to 4
- support: int32 [512, 32], P(('row', 'col')), may hold values from 0 to 511, as said below
- coarse_potential: float32 [512, 128], P(('row', 'col')), may hold values from -4 to 150
Outputs:
- potential_f: float32 [512, 128], P(('row', 'col'))
- potential_g: float32 [512, 128], P(('row', 'col'))
Inputs may be any that keep to these rules, and one draw needn't show every extreme that they name: `support`: each row names 32 different target clusters. The rows of one device's 16 source clusters name, among the 16 target clusters of any one device, exactly 2 different ones. Every target cluster is named by some row.
All inputs are finite; a program needn't handle non-finite values.
Results may differ from a plain program's by a relative error of at most 0.0003.
Values may be sent and summed in bfloat16 or wider, within the bound.
A program may use at most 64 MiB of HBM per device.

v0:
```python
import jax
import jax.numpy as jnp
from jax import lax
from jax.sharding import PartitionSpec as P

CAP = 2
ITERS = 2


epsilon = 0.5
lowest = -1e30


def squares(points):
    wide = points.astype(jnp.float32)
    return jnp.sum(wide * wide, axis=-2)


def cluster_terms(source, source_sq, source_log, tiles, tiles_sq, shifted):
    cross = jnp.einsum("dp,tdq->tpq", source, tiles, preferred_element_type=jnp.float32)
    cost = source_sq[None, :, None] + tiles_sq[:, None, :] - 2.0 * cross
    scores = (shifted[:, None, :] - cost) / epsilon
    peak = jnp.max(scores, axis=(0, 2))
    total = jnp.sum(jnp.exp(scores - peak[None, :, None]), axis=(0, 2))
    potential = -epsilon * (peak + jnp.log(total))
    lifted = potential + epsilon * source_log
    backward = (lifted[None, :, None] - cost) / epsilon
    column_peak = jnp.max(backward, axis=1)
    column_total = jnp.sum(jnp.exp(backward - column_peak[:, None, :]), axis=1)
    return (potential, column_peak, column_total)


def fold_max(old_max, old_sum, new_max, new_sum):
    upper = jnp.maximum(old_max, new_max)
    return (upper, old_sum * jnp.exp(old_max - upper) + new_sum * jnp.exp(new_max - upper))


def body(source_points, target_points, source_mass, target_mass, support, coarse_potential):
    devices = lax.axis_size(("row", "col"))
    local_count = source_points.shape[0]
    slots = CAP
    points = source_points.shape[2]
    owner = support // local_count
    within = support % local_count
    wanted = (
        jnp.zeros((devices, local_count), jnp.int32)
        .at[owner.reshape(-1), within.reshape(-1)]
        .max(1)
    )
    ranking = jnp.cumsum(wanted, axis=1) - 1
    picked = (wanted[:, :, None] == 1) & (ranking[:, :, None] == jnp.arange(slots)[None, None, :])
    request = jnp.sum(jnp.where(picked, jnp.arange(local_count)[None, :, None], 0), axis=1)
    request_used = jnp.any(picked, axis=1).astype(jnp.int32)
    pair_slot = owner * slots + ranking[owner, within]
    asked, asked_used = (
        lax.all_to_all(request, ("row", "col"), split_axis=0, concat_axis=0, tiled=True),
        lax.all_to_all(request_used, ("row", "col"), split_axis=0, concat_axis=0, tiled=True),
    )
    outgoing = target_points[asked]
    arrived = lax.all_to_all(outgoing, ("row", "col"), split_axis=0, concat_axis=0, tiled=True)
    tiles_all = arrived.reshape((devices * slots,) + arrived.shape[2:])
    tiles_sq = squares(tiles_all)
    source_sq = squares(source_points)
    matches = (asked[:, :, None] == jnp.arange(local_count)[None, None, :]) & (
        asked_used[:, :, None] == 1
    )
    potential_g = coarse_potential
    potential_f = jnp.zeros(source_mass.shape, jnp.float32)
    for sweep in range(ITERS):
        sending = (potential_g + epsilon * target_mass)[asked]
        received = lax.all_to_all(sending, ("row", "col"), split_axis=0, concat_axis=0, tiled=True)
        shifted_all = received.reshape(devices * slots, points)

        def visit(carry, item):
            run_max, run_sum = carry
            source, sq_row, log_row, slot_row = item
            potential, column_peak, column_total = cluster_terms(
                source,
                sq_row,
                log_row,
                tiles_all[slot_row],
                tiles_sq[slot_row],
                shifted_all[slot_row],
            )
            upper, summed = fold_max(
                run_max[slot_row], run_sum[slot_row], column_peak, column_total
            )
            return ((run_max.at[slot_row].set(upper), run_sum.at[slot_row].set(summed)), potential)

        start = (
            jnp.full((devices * slots, points), lowest, jnp.float32),
            jnp.zeros((devices * slots, points), jnp.float32),
        )
        (run_max, run_sum), potential_f = lax.scan(
            visit, start, (source_points, source_sq, source_mass, pair_slot)
        )
        partial_max = run_max.reshape(devices, slots, points)
        partial_sum = run_sum.reshape(devices, slots, points)
        peer_max, peer_sum = (
            lax.all_to_all(partial_max, ("row", "col"), split_axis=0, concat_axis=0, tiled=True),
            lax.all_to_all(partial_sum, ("row", "col"), split_axis=0, concat_axis=0, tiled=True),
        )
        masked = jnp.where(matches[..., None], peer_max[:, :, None, :], lowest)
        upper = jnp.max(masked, axis=(0, 1))
        scaled = peer_sum[:, :, None, :] * jnp.exp(
            jnp.minimum(peer_max[:, :, None, :] - upper[None, None], 0.0)
        )
        weight = jnp.where(matches[..., None], scaled, 0.0)
        potential_g = -epsilon * (upper + jnp.log(jnp.sum(weight, axis=(0, 1))))
    return (potential_f, potential_g)


def solution(mesh):
    placed = (
        P(("row", "col"), None, None),
        P(("row", "col"), None, None),
        P(("row", "col"), None),
        P(("row", "col"), None),
        P(("row", "col"), None),
        P(("row", "col"), None),
    )
    return jax.shard_map(
        body,
        mesh=mesh,
        in_specs=placed,
        out_specs=(P(("row", "col"), None), P(("row", "col"), None)),
        check_vma=False,
    )
```

profile of v0, /device:TPU:0, one launch (start us, length us, event | category | flops | bytes accessed | tf_op | source)
XLA Modules:
  0.0 541.7 jit_solution(4589603803563236640)
XLA Ops:
  1.6 25.2 %scatter_fusion = s32[32,16]{0,1:T(8,128)S(1)} fusion(s32[32,16]{0,1:T(8,128)S(1)} %broadcast_in_dim.78, s32[512]{0:T(512)S(1)} %bitcast.96, s32[512]{0:T(512)S(1)} %broadcast.256), kind=kCustom, calls=%fused_computation.18 | custom fusion | flops 512 | bytes 10240 | tf_op jit(solution)/shard_map/scatter-max | solution.py:48
  27.8 7.3 %all-to-all-start = ((s32[32,1,2]{2,1,0:T(1,128)}), s32[32,1,2]{2,1,0:T(1,128)S(1)}, u32[]{:S(2)}, u32[]{:S(2)}) async-start(s32[32,1,2]{2,1,0:T(1,128)} %copy.50), calls=%async_computation | async-start | bytes 32768 | tf_op jit(solution)/shard_map/all_to_all | solution.py:56
  35.9 6.5 %all-to-all-done = s32[32,1,2]{2,1,0:T(1,128)S(1)} async-done(((s32[32,1,2]{2,1,0:T(1,128)}), s32[32,1,2]{2,1,0:T(1,128)S(1)}, u32[]{:S(2)}, u32[]{:S(2)}) %all-to-all-start) | async-done | bytes 288 | tf_op jit(solution)/shard_map/all_to_all | solution.py:56
  46.9 5.2 all-to-all-done.1
  54.8 3.8 gather_fusion.8
  60.2 20.7 %all-to-all-done.3 = bf16[32,2,64,128]{3,2,1,0:T(8,128)(2,1)S(1)} async-done(((bf16[32,2,64,128]{3,2,1,0:T(8,128)(2,1)}), bf16[32,2,64,128]{3,2,1,0:T(8,128)(2,1)S(1)}, u32[]{:S(2)}, u32[]{:S(2)}) %all-to-all-start.3) | async-done | bytes 1048608 | tf_op jit(solution)/shard_map/all_to_all | solution.py:60
  80.9 3.5 all-to-all-start.2
  84.8 6.9 %all-to-all-done.2 = f32[32,2,128]{2,1,0:T(2,128)S(1)} async-done(((f32[32,2,128]{2,1,0:T(2,128)}), f32[32,2,128]{2,1,0:T(2,128)S(1)}, u32[]{:S(2)}, u32[]{:S(2)}) %all-to-all-start.2) | async-done | bytes 32800 | tf_op jit(solution)/shard_map/all_to_all | solution.py:71
  92.9 204.7 %while.26 = (s32[]{:T(128)}, f32[64,128]{1,0:T(8,128)}, f32[64,128]{1,0:T(8,128)}, s32[16,32]{1,0:T(8,128)S(1)}, f32[64,128]{1,0:T(8,128)S(1)}, /*index=5*/f32[1...) while((s32[]{:T(128)}, f32[64,128]{1,0:T(8,128)}, ...), condition=%wide.region_13.14_spmd, body=%wide.region_6.13_spmd.sunk | while | flops 76043616 | bytes 10370045 | solution.py:94
  139.3 2.8 scatter_custom_fusion.20
  177.7 2.8 scatter_custom_fusion.20
  203.3 2.8 scatter_custom_fusion.20
  300.3 7.1 %all-to-all-done.4 = f32[32,2,128]{2,1,0:T(2,128)S(1)} async-done(((f32[32,2,128]{2,1,0:T(2,128)}), f32[32,2,128]{2,1,0:T(2,128)S(1)}, u32[]{:S(2)}, u32[]{:S(2)}) %all-to-all-start.4) | async-done | bytes 32800 | tf_op jit(solution)/shard_map/all_to_all | solution.py:100
  310.2 7.0 %all-to-all-done.5 = f32[32,2,128]{2,1,0:T(2,128)S(1)} async-done(((f32[32,2,128]{2,1,0:T(2,128)}), f32[32,2,128]{2,1,0:T(2,128)S(1)}, u32[]{:S(2)}, u32[]{:S(2)}) %all-to-all-start.5) | async-done | bytes 32800 | tf_op jit(solution)/shard_map/all_to_all | solution.py:101
  321.2 7.2 %all-to-all-done.6 = f32[32,2,128]{2,1,0:T(2,128)S(1)} async-done(((f32[32,2,128]{2,1,0:T(2,128)}), f32[32,2,128]{2,1,0:T(2,128)S(1)}, u32[]{:S(2)}, u32[]{:S(2)}) %all-to-all-start.6) | async-done | bytes 32800 | tf_op jit(solution)/shard_map/all_to_all | solution.py:71
  329.1 193.0 %while.27 = (s32[]{:T(128)}, f32[64,128]{1,0:T(8,128)S(1)}, f32[64,128]{1,0:T(8,128)}, f32[16,128]{1,0:T(8,128)}, s32[16,32]{1,0:T(8,128)S(1)}, /*index=5*/f32[6...) while((s32[]{:T(128)}, f32[64,128]{1,0:T(8,128)S(1)}, ...), condition=%wide.region_23.24_spmd, body=%wide.region_16.23_spmd.sunk | while | flops 76043616 | bytes 10371601 | solution.py:94
  348.4 2.8 scatter_custom_fusion.24
  360.5 2.8 scatter_custom_fusion.24
  372.6 2.8 scatter_custom_fusion.24
  396.7 2.8 scatter_custom_fusion.24
  457.0 2.8 scatter_custom_fusion.24
  469.0 2.8 scatter_custom_fusion.24
  522.1 8.9 %all_to_all.53 = f32[32,2,128]{2,1,0:T(2,128)S(1)} all-to-all(f32[32,2,128]{2,1,0:T(2,128)S(1)} %bitcast.97), channel_id=1, replica_groups=mesh['row'=8,'col'=4] {'row','col'}, dimensions={0} | all-to-all | bytes 65536 | tf_op jit(solution)/shard_map/all_to_all | solution.py:100
  533.8 7.0 %all-to-all-done.8 = f32[32,2,128]{2,1,0:T(2,128)S(1)} async-done(((f32[32,2,128]{2,1,0:T(2,128)}), f32[32,2,128]{2,1,0:T(2,128)S(1)}, u32[]{:S(2)}, u32[]{:S(2)}) %all-to-all-start.8) | async-done | bytes 32800 | tf_op jit(solution)/shard_map/all_to_all | solution.py:101
  (516 shorter events, 397.8 us)
Async XLA Ops:
  0.6 44.6 %copy-start = (bf16[16,64,128]{2,1,0:T(8,128)(2,1)S(1)}, bf16[16,64,128]{2,1,0:T(8,128)(2,1)}, u32[]{:S(2)}) copy-start(bf16[16,64,128]{2,1,0:T(8,128)(2,1)} %param.11) | copy-start | bytes 786436
  27.8 14.5 %all-to-all-start = ((s32[32,1,2]{2,1,0:T(1,128)}), s32[32,1,2]{2,1,0:T(1,128)S(1)}, u32[]{:S(2)}, u32[]{:S(2)}) async-start(s32[32,1,2]{2,1,0:T(1,128)} %copy.50), calls=%async_computation | async-start | bytes 32768 | tf_op jit(solution)/shard_map/all_to_all | solution.py:56
  42.3 9.7 %all-to-all-start.1 = ((s32[32,1,2]{2,1,0:T(1,128)}), s32[32,1,2]{2,1,0:T(1,128)S(1)}, u32[]{:S(2)}, u32[]{:S(2)}) async-start(s32[32,1,2]{2,1,0:T(1,128)} %copy.53), calls=%async_computation.1 | async-start | bytes 32768 | tf_op jit(solution)/shard_map/all_to_all | solution.py:57
  52.1 28.8 %all-to-all-start.3 = ((bf16[32,2,64,128]{3,2,1,0:T(8,128)(2,1)}), bf16[32,2,64,128]{3,2,1,0:T(8,128)(2,1)S(1)}, u32[]{:S(2)}, u32[]{:S(2)}) async-start(bf16[32,2,64,128]{3,2,1,0:T(8,128)(2,1)} %bitcast.23), calls=%async_computation.3 | async-start | bytes 2097152 | tf_op jit(solution)/shard_map/all_to_all | solution.py:60
  54.8 3.9 copy-start.1
  54.8 3.9 copy-start.2
  54.8 4.0 copy-start.3
  54.8 4.0 copy-start.4
  80.9 10.8 %all-to-all-start.2 = ((f32[32,2,128]{2,1,0:T(2,128)}), f32[32,2,128]{2,1,0:T(2,128)S(1)}, u32[]{:S(2)}, u32[]{:S(2)}) async-start(f32[32,2,128]{2,1,0:T(2,128)} %bitcast.21), calls=%async_computation.2 | async-start | bytes 65536 | tf_op jit(solution)/shard_map/all_to_all | solution.py:71
  297.6 9.8 %all-to-all-start.4 = ((f32[32,2,128]{2,1,0:T(2,128)}), f32[32,2,128]{2,1,0:T(2,128)S(1)}, u32[]{:S(2)}, u32[]{:S(2)}) async-start(f32[32,2,128]{2,1,0:T(2,128)} %bitcast.26), calls=%async_computation.4 | async-start | bytes 65536 | tf_op jit(solution)/shard_map/all_to_all | solution.py:100
  307.4 9.8 %all-to-all-start.5 = ((f32[32,2,128]{2,1,0:T(2,128)}), f32[32,2,128]{2,1,0:T(2,128)S(1)}, u32[]{:S(2)}, u32[]{:S(2)}) async-start(f32[32,2,128]{2,1,0:T(2,128)} %bitcast.27), calls=%async_computation.5 | async-start | bytes 65536 | tf_op jit(solution)/shard_map/all_to_all | solution.py:101
  318.7 9.8 %all-to-all-start.6 = ((f32[32,2,128]{2,1,0:T(2,128)}), f32[32,2,128]{2,1,0:T(2,128)S(1)}, u32[]{:S(2)}, u32[]{:S(2)}) async-start(f32[32,2,128]{2,1,0:T(2,128)} %bitcast.28), calls=%async_computation.6 | async-start | bytes 65536 | tf_op jit(solution)/shard_map/all_to_all | solution.py:71
  531.0 9.8 %all-to-all-start.8 = ((f32[32,2,128]{2,1,0:T(2,128)}), f32[32,2,128]{2,1,0:T(2,128)S(1)}, u32[]{:S(2)}, u32[]{:S(2)}) async-start(f32[32,2,128]{2,1,0:T(2,128)} %bitcast.31), calls=%async_computation.8 | async-start | bytes 65536 | tf_op jit(solution)/shard_map/all_to_all | solution.py:101
where the time goes:
time: 548 us; the launch traced here: 542 us
  other arithmetic  269 us (49%)
  local copies, waits for them, and re-layouts  121 us (22%)
  waiting for transfers between devices  67.7 us (12%)
  matrix products  46.5 us (8%)
  starting transfers between devices  26.3 us (5%)
  blocking collectives  8.93 us (2%)
    scatter x32, other arithmetic, visit(): run_sum.at[slot_row].set(summed)  89.3 us
    dot_general x32, matrix products, cluster_terms(): jnp.einsum('dp,tdq->tpq', source, tiles, preferred_element_type=jnp.float32)  46.5 us
    scatter x32, other arithmetic, visit(): run_max.at[slot_row].set(upper)  42.7 us
    reduce_sum x32, other arithmetic, cluster_terms(): column_total = jnp.sum(jnp.exp(backward - column_peak[:, None, :]), axis=1)  42.4 us
    gather x32, local copies, waits for them, and re-layouts, visit(): run_max[slot_row]  30.5 us
    another operation x1, other arithmetic, body(): wanted = jnp.zeros((devices, local_count), jnp.int32).at[owner.reshape(-1...  25.2 us
    reduce_sum x32, other arithmetic, cluster_terms(): total = jnp.sum(jnp.exp(scores - peak[None, :, None]), axis=(0, 2))  23.7 us
    dynamic_update_slice x16, local copies, waits for them, and re-layouts, body(): lax.scan(visit, start, (source_points, source_sq, source_mass, pair_slot))  20.8 us
  transfers between devices with their start and end apart: 8, of which 8 were waited for; matrix products, arithmetic and copies ran while one was open for 2% of the time, Pallas kernels for 0%

commit v1 on v0

v1 whole, which is shorter than its diff:
```python
import jax
import jax.numpy as jnp
from jax import lax
from jax.experimental import pallas as pl
from jax.experimental.pallas import tpu as pltpu
from jax.sharding import PartitionSpec as P

CAP = 2
ITERS = 2
AXES = ("row", "col")
GROUP = 4


epsilon = 0.5
lowest = -1e30


def squares(points):
    wide = points.astype(jnp.float32)
    return jnp.sum(wide * wide, axis=-2)


def pieces(row, depth):
    high = row.astype(jnp.bfloat16).astype(jnp.float32)
    rest = row - high
    middle = rest.astype(jnp.bfloat16).astype(jnp.float32)
    low = rest - middle
    index = lax.broadcasted_iota(jnp.int32, (depth, row.shape[1]), 0)
    return jnp.where(
        index == 0, high, jnp.where(index == 1, middle, jnp.where(index == 2, low, 0.0))
    )


def ones_rows(depth, points):
    index = lax.broadcasted_iota(jnp.int32, (depth, points), 0)
    return jnp.where(index < 3, 1.0, 0.0)


def fold(old_max, old_sum, scores):
    rows, lanes = scores.shape
    blocks = scores.reshape(rows // 8, 8, lanes)
    upper = jnp.maximum(old_max, jnp.max(blocks, axis=0))
    total = old_sum * jnp.exp(old_max - upper) + jnp.sum(jnp.exp(blocks - upper[None]), axis=0)
    return upper, total


def sweep_kernel(
    slots_ref, source_ref, mass_ref, tiles_ref, u_ref, row_ref, column_ref,
    tile_forward, tile_backward, run_max, run_sum,
):
    clusters, features, points = source_ref.shape
    slots = tiles_ref.shape[0]
    entries = slots_ref.shape[1]
    spare = tile_forward.shape[2] - features
    ones = ones_rows(spare, points)

    def prepare(slot, carry):
        tile = tiles_ref[slot].astype(jnp.float32)
        extra = pieces(u_ref[pl.ds(slot, 1), :], spare)
        tile_forward[slot] = jnp.concatenate([4.0 * tile, extra], axis=0).T.astype(jnp.bfloat16)
        tile_backward[slot] = jnp.concatenate([tile, ones], axis=0).astype(jnp.bfloat16)
        run_max[slot] = jnp.full((8, points), lowest, jnp.float32)
        run_sum[slot] = jnp.zeros((8, points), jnp.float32)
        return carry

    lax.fori_loop(0, slots, prepare, 0, unroll=4)

    def visit(cluster, carry):
        source = source_ref[cluster].astype(jnp.float32)
        right = jnp.concatenate([source, ones], axis=0).astype(jnp.bfloat16)

        def forward(step, state):
            lhs = jnp.concatenate(
                [tile_forward[slots_ref[cluster, step * GROUP + lane]] for lane in range(GROUP)],
                axis=0,
            )
            return fold(*state, jnp.dot(lhs, right, preferred_element_type=jnp.float32))

        start = (
            jnp.full((8, points), lowest, jnp.float32),
            jnp.zeros((8, points), jnp.float32),
        )
        upper, total = lax.fori_loop(0, entries // GROUP, forward, start, unroll=True)
        peak = jnp.max(upper, axis=0, keepdims=True)
        total = jnp.sum(total * jnp.exp(upper - peak), axis=0, keepdims=True)
        level = peak + jnp.log(total)
        row_ref[pl.ds(cluster, 1), :] = level
        extra = pieces(mass_ref[pl.ds(cluster, 1), :] - level, spare)
        left = jnp.concatenate([4.0 * source, extra], axis=0).T.astype(jnp.bfloat16)

        def backward(step, state):
            chosen = [slots_ref[cluster, step * GROUP + lane] for lane in range(GROUP)]
            held = [(run_max[slot], run_sum[slot]) for slot in chosen]
            rhs = jnp.concatenate([tile_backward[slot] for slot in chosen], axis=1)
            scores = jnp.dot(left, rhs, preferred_element_type=jnp.float32)
            fresh = [
                fold(*held[lane], scores[:, lane * points : (lane + 1) * points])
                for lane in range(GROUP)
            ]
            for slot, (new_max, new_sum) in zip(chosen, fresh):
                run_max[slot] = new_max
                run_sum[slot] = new_sum
            return state

        lax.fori_loop(0, entries // GROUP, backward, 0, unroll=True)
        return carry

    lax.fori_loop(0, clusters, visit, 0)
    upper = run_max[...]
    peak = jnp.max(upper, axis=1, keepdims=True)
    total = jnp.sum(run_sum[...] * jnp.exp(upper - peak), axis=1)
    column_ref[...] = peak[:, 0] + jnp.log(total)


def sweep_call(slot_list, source, mass, tiles, u):
    clusters, features, points = source.shape
    slots = tiles.shape[0]
    depth = 2 * features
    vmem = pl.BlockSpec(memory_space=pltpu.VMEM)
    pairs = clusters * slot_list.shape[1]
    return pl.pallas_call(
        sweep_kernel,
        out_shape=(
            jax.ShapeDtypeStruct((clusters, points), jnp.float32),
            jax.ShapeDtypeStruct((slots, points), jnp.float32),
        ),
        in_specs=[pl.BlockSpec(memory_space=pltpu.SMEM), vmem, vmem, vmem, vmem],
        out_specs=(vmem, vmem),
        scratch_shapes=[
            pltpu.VMEM((slots, points, depth), jnp.bfloat16),
            pltpu.VMEM((slots, depth, points), jnp.bfloat16),
            pltpu.VMEM((slots, 8, points), jnp.float32),
            pltpu.VMEM((slots, 8, points), jnp.float32),
        ],
        cost_estimate=pl.CostEstimate(
            flops=4 * pairs * points * points * depth,
            transcendentals=2 * pairs * points * points,
            bytes_accessed=2 * slots * features * points,
        ),
        name="sweep",
    )(slot_list, source, mass, tiles, u)


def exchange(array):
    return lax.all_to_all(array, AXES, split_axis=0, concat_axis=0, tiled=True)


def body(source_points, target_points, source_mass, target_mass, support, coarse_potential):
    devices = lax.axis_size(AXES)
    local_count, features, points = source_points.shape
    owner = support // local_count
    within = support % local_count
    flat_owner, flat_within = owner.reshape(-1), within.reshape(-1)
    named = flat_owner[None, :] == jnp.arange(devices, dtype=jnp.int32)[:, None]
    first = jnp.min(jnp.where(named, flat_within[None, :], local_count), axis=1)
    second = jnp.max(jnp.where(named, flat_within[None, :], -1), axis=1)
    request = jnp.stack([first, second], axis=1)
    first_of = jnp.sum(jnp.where(named, first[:, None], 0), axis=0).reshape(owner.shape)
    slot_list = (owner * CAP + (within > first_of).astype(jnp.int32)).astype(jnp.int32)
    asked = exchange(request)

    target_sq = squares(target_points)
    source_sq = squares(source_points)
    u = 2.0 * (coarse_potential - target_sq) + target_mass
    tiles = exchange(target_points[asked]).reshape(devices * CAP, features, points)
    flat_asked = asked.reshape(-1)
    matches = flat_asked[:, None] == jnp.arange(local_count, dtype=jnp.int32)[None, :]
    for sweep in range(ITERS):
        sending = jnp.sum(jnp.where(matches[:, :, None], u[None, :, :], 0.0), axis=1)
        received = exchange(sending.reshape(devices, CAP, points)).reshape(devices * CAP, points)
        level, column = sweep_call(slot_list, source_points, source_mass, tiles, received)
        peer = exchange(column.reshape(devices, CAP, points)).reshape(devices * CAP, points)
        masked = jnp.where(matches[:, :, None], peer[:, None, :], lowest)
        upper = jnp.max(masked, axis=0)
        total = jnp.sum(jnp.exp(masked - upper[None]), axis=0)
        column_level = upper + jnp.log(total)
        u = target_mass - column_level
    return (source_sq - 0.5 * level, target_sq - 0.5 * column_level)


def solution(mesh):
    placed = (
        P(AXES, None, None),
        P(AXES, None, None),
        P(AXES, None),
        P(AXES, None),
        P(AXES, None),
        P(AXES, None),
    )
    return jax.shard_map(
        body,
        mesh=mesh,
        in_specs=placed,
        out_specs=(P(AXES, None), P(AXES, None)),
        check_vma=False,
    )
```

time: 548 us -> 143 us (0.26); the launches traced: 542 us -> 142 us
  other arithmetic: 269 us -> 7.19 us
  local copies, waits for them, and re-layouts: 121 us -> 6.21 us
  Pallas kernels: 0 us -> 49.3 us
  matrix products: 46.5 us -> 0 us
  waiting for transfers between devices: 67.7 us -> 50.3 us
  starting transfers between devices: 26.3 us -> 17.8 us
    scatter x64 -> x0, other arithmetic: 132 us -> none  [the longest x32 89.3 us: visit(): run_sum.at[slot_row].set(summed)]
    gather x133 -> x1, local copies, waits for them, and re-layouts: 95.7 us -> 1.67 us  [body(): target_points[asked]]
    reduce_sum x67 -> x5, other arithmetic: 66.5 us -> 2.17 us  [the longest x2 1.66 us: body(): jnp.sum(jnp.where(matches[:, :, None], u[None, :, :], 0.0), axis=1)]
    pallas_call x0 -> x2, Pallas kernels: none -> 49.3 us  [sweep_call(): pl.pallas_call(sweep_kernel, out_shape=(jax.ShapeDtypeStruct((clusters, p...]
    dot_general x32 -> x0, matrix products: 46.5 us -> none  [cluster_terms(): jnp.einsum('dp,tdq->tpq', source, tiles, preferred_element_type=jnp.float32)]
    another operation x2 -> x0, other arithmetic: 25.3 us -> none  [the longest x1 25.2 us: body(): wanted = jnp.zeros((devices, local_count), jnp.int32).at[owner.reshape(-1...]
    dynamic_update_slice x16 -> x0, local copies, waits for them, and re-layouts: 20.8 us -> none  [body(): lax.scan(visit, start, (source_points, source_sq, source_mass, pair_slot))]
    reduce_max x34 -> x3, other arithmetic: 20.1 us -> 0.53 us  [the longest x2 0.4 us: body(): upper = jnp.max(masked, axis=0)]
  transfers between devices with their start and end apart: 8 -> 5, of which waited for: 8 -> 5; matrix products, arithmetic and copies ran while one was open for 2% -> 3% of each run, Pallas kernels for 0% -> 0%
where the time goes in v1:
time: 143 us; the launch traced here: 142 us
  waiting for transfers between devices  50.3 us (35%)
  Pallas kernels  49.3 us (34%)
  starting transfers between devices  17.8 us (12%)
  blocking collectives  10.8 us (8%)
  other arithmetic  7.19 us (5%)
  local copies, waits for them, and re-layouts  6.21 us (4%)
    all_to_all x5, waiting for transfers between devices, exchange(): return lax.all_to_all(array, AXES, split_axis=0, concat_axis=0, tiled=True)  50.3 us
    pallas_call x2, Pallas kernels, sweep_call(): pl.pallas_call(sweep_kernel, out_shape=(jax.ShapeDtypeStruct((clusters, p...  49.3 us
    all_to_all x5, starting transfers between devices, exchange(): return lax.all_to_all(array, AXES, split_axis=0, concat_axis=0, tiled=True)  17.8 us
    all_to_all x1, blocking collectives, exchange(): return lax.all_to_all(array, AXES, split_axis=0, concat_axis=0, tiled=True)  10.8 us
  transfers between devices with their start and end apart: 5, of which 5 were waited for; matrix products, arithmetic and copies ran while one was open for 3% of the time, Pallas kernels for 0%

profile of v1, /device:TPU:0, one launch (start us, length us, event | category | flops | bytes accessed | tf_op | source)
XLA Modules:
  0.0 142.4 jit_solution(3212948128075864113)
XLA Ops:
  0.6 0.7 add_select_fusion.1
  1.6 0.7 copy.15
  2.3 7.3 %all-to-all-start = ((s32[32,1,2]{2,1,0:T(1,128)}), s32[32,1,2]{2,1,0:T(1,128)S(1)}, u32[]{:S(2)}, u32[]{:S(2)}) async-start(s32[32,1,2]{2,1,0:T(1,128)} %copy.15), calls=%async_computation | async-start | bytes 32768 | tf_op jit(solution)/shard_map/all_to_all | solution.py:145
  9.7 1.1 multiply_reduce_fusion
  10.8 6.0 %all-to-all-done = s32[32,1,2]{2,1,0:T(1,128)S(1)} async-done(((s32[32,1,2]{2,1,0:T(1,128)}), s32[32,1,2]{2,1,0:T(1,128)S(1)}, u32[]{:S(2)}, u32[]{:S(2)}) %all-to-all-start) | async-done | bytes 288 | tf_op jit(solution)/shard_map/all_to_all | solution.py:145
  17.6 0.7 reduce.3
  18.5 0.8 select_reduce_fusion.3
  19.4 2.6 %all-to-all-start.2 = ((f32[32,2,128]{2,1,0:T(2,128)}), f32[32,2,128]{2,1,0:T(2,128)S(1)}, u32[]{:S(2)}, u32[]{:S(2)}) async-start(f32[32,2,128]{2,1,0:T(2,128)} %bitcast.6), calls=%async_computation.2 | async-start | bytes 65536 | tf_op jit(solution)/shard_map/all_to_all | solution.py:145
  21.9 1.7 %gather_fusion = bf16[64,64,128]{2,1,0:T(8,128)(2,1)} fusion(bf16[16,64,128]{2,1,0:T(8,128)(2,1)S(1)} %copy-done, s32[1024]{0:T(1024)S(1)} %pad_clamp_fusion), kind=kCustom, calls=%fused_computation | custom fusion | bytes 2097408 | tf_op jit(solution)/shard_map/gather | solution.py:165
  23.6 5.6 %all-to-all-done.2 = f32[32,2,128]{2,1,0:T(2,128)S(1)} async-done(((f32[32,2,128]{2,1,0:T(2,128)}), f32[32,2,128]{2,1,0:T(2,128)S(1)}, u32[]{:S(2)}, u32[]{:S(2)}) %all-to-all-start.2) | async-done | bytes 32800 | tf_op jit(solution)/shard_map/all_to_all | solution.py:145
  29.8 2.6 %all-to-all-start.1 = ((bf16[32,2,64,128]{3,2,1,0:T(8,128)(2,1)}), bf16[32,2,64,128]{3,2,1,0:T(8,128)(2,1)S(1)}, u32[]{:S(2)}, u32[]{:S(2)}) async-start(bf16[32,2,64,128]{3,2,1,0:T(8,128)(2,1)} %bitcast.4), calls=%async_computation.1 | async-start | bytes 2097152 | tf_op jit(solution)/shard_map/all_to_all | solution.py:145
  33.1 0.6 convert_add_fusion.slots_ref
  33.7 24.9 %all-to-all-done.1 = bf16[32,2,64,128]{3,2,1,0:T(8,128)(2,1)S(1)} async-done(((bf16[32,2,64,128]{3,2,1,0:T(8,128)(2,1)}), bf16[32,2,64,128]{3,2,1,0:T(8,128)(2,1)S(1)}, u32[]{:S(2)}, u32[]{:S(2)}) %all-to-all-start.1) | async-done | bytes 1048608 | tf_op jit(solution)/shard_map/all_to_all | solution.py:145
  58.6 1.0 copy-done.1
  59.6 24.7 %sweep.2 = (f32[16,128]{1,0:T(8,128)}, f32[64,128]{1,0:T(8,128)}) custom-call(s32[16,32]{1,0:T(8,128)} %convert_add_fusion.slots_ref, bf16[16,64,128]{2,1,0:T(8,128)(2,1)} %source_ref.3, f32[16,128]{1,0:T(8,128)} %mass_ref.3, bf16[64,64,128]{2,1,0:T(8,128)(2,1)} %bitcast.18, f32[64,128]{1,0:T(8,128)} %bitcast.24), custom_call_target="tpu_custom_call" | custom-call | flops 4294967296 | bytes 1048576 | tf_op jit(solution)/shard_map/sweep/pallas_call | solution.py:121
  84.3 10.8 %all_to_all.37 = f32[32,2,128]{2,1,0:T(2,128)S(1)} all-to-all(f32[32,2,128]{2,1,0:T(2,128)} %bitcast.27), channel_id=1, replica_groups=mesh['row'=8,'col'=4] {'row','col'}, dimensions={0} | all-to-all | bytes 65536 | tf_op jit(solution)/shard_map/all_to_all | solution.py:145
  95.5 0.8 select_reduce_fusion.2
  96.4 2.6 %all-to-all-start.4 = ((f32[32,2,128]{2,1,0:T(2,128)}), f32[32,2,128]{2,1,0:T(2,128)S(1)}, u32[]{:S(2)}, u32[]{:S(2)}) async-start(f32[32,2,128]{2,1,0:T(2,128)} %bitcast.10), calls=%async_computation.4 | async-start | bytes 65536 | tf_op jit(solution)/shard_map/all_to_all | solution.py:145
  99.0 7.2 %all-to-all-done.4 = f32[32,2,128]{2,1,0:T(2,128)S(1)} async-done(((f32[32,2,128]{2,1,0:T(2,128)}), f32[32,2,128]{2,1,0:T(2,128)S(1)}, u32[]{:S(2)}, u32[]{:S(2)}) %all-to-all-start.4) | async-done | bytes 32800 | tf_op jit(solution)/shard_map/all_to_all | solution.py:145
  106.8 24.7 %sweep.3 = (f32[16,128]{1,0:T(8,128)}, f32[64,128]{1,0:T(8,128)}) custom-call(s32[16,32]{1,0:T(8,128)} %convert_add_fusion.slots_ref, bf16[16,64,128]{2,1,0:T(8,128)(2,1)} %source_ref.3, f32[16,128]{1,0:T(8,128)} %mass_ref.3, bf16[64,64,128]{2,1,0:T(8,128)(2,1)} %bitcast.19, f32[64,128]{1,0:T(8,128)} %bitcast.25), custom_call_target="tpu_custom_call" | custom-call | flops 4294967296 | bytes 1048576 | tf_op jit(solution)/shard_map/sweep/pallas_call | solution.py:121
  131.5 2.7 %all-to-all-start.5 = ((f32[32,2,128]{2,1,0:T(2,128)}), f32[32,2,128]{2,1,0:T(2,128)S(1)}, u32[]{:S(2)}, u32[]{:S(2)}) async-start(f32[32,2,128]{2,1,0:T(2,128)} %bitcast.26), calls=%async_computation.5 | async-start | bytes 65536 | tf_op jit(solution)/shard_map/all_to_all | solution.py:145
  134.2 0.6 multiply_subtract_fusion.1
  134.8 6.6 %all-to-all-done.5 = f32[32,2,128]{2,1,0:T(2,128)S(1)} async-done(((f32[32,2,128]{2,1,0:T(2,128)}), f32[32,2,128]{2,1,0:T(2,128)S(1)}, u32[]{:S(2)}, u32[]{:S(2)}) %all-to-all-start.5) | async-done | bytes 32800 | tf_op jit(solution)/shard_map/all_to_all | solution.py:145
  141.8 0.6 multiply_subtract_fusion
  (38 shorter events, 4.1 us)
Async XLA Ops:
  2.3 8.4 %copy-start.8 = (f32[16,128]{1,0:T(8,128)S(1)}, f32[16,128]{1,0:T(8,128)}, u32[]{:S(2)}) copy-start(f32[16,128]{1,0:T(8,128)} %param.11) | copy-start | bytes 24580
  2.3 14.5 %all-to-all-start = ((s32[32,1,2]{2,1,0:T(1,128)}), s32[32,1,2]{2,1,0:T(1,128)S(1)}, u32[]{:S(2)}, u32[]{:S(2)}) async-start(s32[32,1,2]{2,1,0:T(1,128)} %copy.15), calls=%async_computation | async-start | bytes 32768 | tf_op jit(solution)/shard_map/all_to_all | solution.py:145
  9.7 1.1 copy-start.6
  9.7 12.3 %copy-start = (bf16[16,64,128]{2,1,0:T(8,128)(2,1)S(1)}, bf16[16,64,128]{2,1,0:T(8,128)(2,1)}, u32[]{:S(2)}) copy-start(bf16[16,64,128]{2,1,0:T(8,128)(2,1)} %param.7) | copy-start | bytes 786436
  19.4 9.8 %all-to-all-start.2 = ((f32[32,2,128]{2,1,0:T(2,128)}), f32[32,2,128]{2,1,0:T(2,128)S(1)}, u32[]{:S(2)}, u32[]{:S(2)}) async-start(f32[32,2,128]{2,1,0:T(2,128)} %bitcast.6), calls=%async_computation.2 | async-start | bytes 65536 | tf_op jit(solution)/shard_map/all_to_all | solution.py:145
  29.2 0.6 copy-start.4
  29.8 28.8 %all-to-all-start.1 = ((bf16[32,2,64,128]{3,2,1,0:T(8,128)(2,1)}), bf16[32,2,64,128]{3,2,1,0:T(8,128)(2,1)S(1)}, u32[]{:S(2)}, u32[]{:S(2)}) async-start(bf16[32,2,64,128]{3,2,1,0:T(8,128)(2,1)} %bitcast.4), calls=%async_computation.1 | async-start | bytes 2097152 | tf_op jit(solution)/shard_map/all_to_all | solution.py:145
  32.4 0.7 copy-start.3
  58.6 1.0 copy-start.1
  84.3 14.7 %copy-start.2 = (bf16[16,64,128]{2,1,0:T(8,128)(2,1)S(1)}, bf16[16,64,128]{2,1,0:T(8,128)(2,1)}, u32[]{:S(2)}) copy-start(bf16[16,64,128]{2,1,0:T(8,128)(2,1)} %source_ref.3) | copy-start | bytes 786436
  96.4 9.8 %all-to-all-start.4 = ((f32[32,2,128]{2,1,0:T(2,128)}), f32[32,2,128]{2,1,0:T(2,128)S(1)}, u32[]{:S(2)}, u32[]{:S(2)}) async-start(f32[32,2,128]{2,1,0:T(2,128)} %bitcast.10), calls=%async_computation.4 | async-start | bytes 65536 | tf_op jit(solution)/shard_map/all_to_all | solution.py:145
  106.2 0.6 copy-start.5
  131.5 2.7 %copy-start.7 = (f32[16,128]{1,0:T(8,128)S(1)}, f32[16,128]{1,0:T(8,128)}, u32[]{:S(2)}) copy-start(f32[16,128]{1,0:T(8,128)} %get-tuple-element.6) | copy-start | bytes 24580
  131.5 9.9 %all-to-all-start.5 = ((f32[32,2,128]{2,1,0:T(2,128)}), f32[32,2,128]{2,1,0:T(2,128)S(1)}, u32[]{:S(2)}, u32[]{:S(2)}) async-start(f32[32,2,128]{2,1,0:T(2,128)} %bitcast.26), calls=%async_computation.5 | async-start | bytes 65536 | tf_op jit(solution)/shard_map/all_to_all | solution.py:145

commit v2 on v1

--- a/solution.py
+++ b/solution.py
@@ -1,3 +1,5 @@
+import functools
+
 import jax
 import jax.numpy as jnp
 from jax import lax
@@ -9,6 +11,7 @@
 ITERS = 2
 AXES = ("row", "col")
 GROUP = 4
+MESH = pl.DeviceIdType.MESH
 
 
 epsilon = 0.5
@@ -141,8 +144,125 @@
     )(slot_list, source, mass, tiles, u)
 
 
-def exchange(array):
-    return lax.all_to_all(array, AXES, split_axis=0, concat_axis=0, tiled=True)
+def place():
+    rows, columns = lax.axis_size("row"), lax.axis_size("col")
+    return lax.axis_index("row") * columns + lax.axis_index("col"), rows * columns, columns
+
+
+def peer_of(step):
+    me, devices, columns = place()
+    peer = lax.rem(me + step, devices)
+    return peer, (lax.div(peer, columns), lax.rem(peer, columns))
+
+
+def greet():
+    devices = place()[1]
+    barrier = pltpu.get_barrier_semaphore()
+
+    def signal(step, carry):
+        pl.semaphore_signal(barrier, inc=1, device_id=peer_of(step)[1], device_id_type=MESH)
+        return carry
+
+    lax.fori_loop(1, devices, signal, 0)
+    pl.semaphore_wait(barrier, devices - 1)
+
+
+def send_all(sources, targets, send_sem, recv_sem, first):
+    me, devices, _ = place()
+
+    def send(step, carry):
+        peer, where = peer_of(step)
+        for index, (source, target) in enumerate(zip(sources, targets)):
+            pltpu.make_async_remote_copy(
+                src_ref=source.at[peer],
+                dst_ref=target.at[me],
+                send_sem=send_sem.at[first + index],
+                recv_sem=recv_sem.at[first + index],
+                device_id=where,
+                device_id_type=MESH,
+            ).start()
+        return carry
+
+    lax.fori_loop(1, devices, send, 0)
+    for source, target in zip(sources, targets):
+        target[me] = source[me]
+
+
+def wait_all(refs, sems, first):
+    devices = place()[1]
+    for index, ref in enumerate(refs):
+        blocks = ref.at[pl.ds(0, devices - 1)]
+        pltpu.make_async_copy(blocks, blocks, sems.at[first + index]).wait()
+
+
+def exchange_kernel(count, *refs):
+    sources, targets = refs[:count], refs[count : 2 * count]
+    send_sem, recv_sem = refs[2 * count :]
+    greet()
+    send_all(sources, targets, send_sem, recv_sem, 0)
+    wait_all(targets, recv_sem, 0)
+    wait_all(sources, send_sem, 0)
+
+
+def exchange(arrays, collective_id):
+    count = len(arrays)
+    vmem = pl.BlockSpec(memory_space=pltpu.VMEM)
+    return pl.pallas_call(
+        functools.partial(exchange_kernel, count),
+        out_shape=tuple(jax.ShapeDtypeStruct(array.shape, array.dtype) for array in arrays),
+        in_specs=[vmem] * count,
+        out_specs=(vmem,) * count,
+        scratch_shapes=[pltpu.SemaphoreType.DMA((count,)), pltpu.SemaphoreType.DMA((count,))],
+        compiler_params=pltpu.CompilerParams(collective_id=collective_id, has_side_effects=True),
+        name="exchange" + str(collective_id),
+    )(*arrays)
+
+
+def combined(asked, parts, cluster):
+    masked = jnp.where(asked == cluster, parts, lowest)
+    upper = jnp.max(jnp.max(masked, axis=0), axis=0, keepdims=True)
+    total = jnp.sum(jnp.sum(jnp.exp(masked - upper[None]), axis=0), axis=0, keepdims=True)
+    return upper + jnp.log(total)
+
+
+def turn_kernel(column_ref, asked_ref, mass_ref, u_ref, parts_ref, outgoing_ref, send_sem, recv_sem):
+    greet()
+    send_all([column_ref], [parts_ref], send_sem, recv_sem, 0)
+    wait_all([parts_ref], recv_sem, 0)
+    asked, parts = asked_ref[...], parts_ref[...]
+
+    outgoing = jnp.zeros(parts.shape, jnp.float32)
+    for cluster in range(mass_ref.shape[0]):
+        row = mass_ref[cluster : cluster + 1, :] - combined(asked, parts, cluster)
+        outgoing = jnp.where(asked == cluster, row[None], outgoing)
+    outgoing_ref[...] = outgoing
+    send_all([outgoing_ref], [u_ref], send_sem, recv_sem, 1)
+    wait_all([u_ref], recv_sem, 1)
+    wait_all([column_ref, outgoing_ref], send_sem, 0)
+
+
+def finish_kernel(column_ref, asked_ref, level_ref, parts_ref, send_sem, recv_sem):
+    greet()
+    send_all([column_ref], [parts_ref], send_sem, recv_sem, 0)
+    wait_all([parts_ref], recv_sem, 0)
+    asked, parts = asked_ref[...], parts_ref[...]
+    for cluster in range(level_ref.shape[0]):
+        level_ref[cluster : cluster + 1, :] = combined(asked, parts, cluster)
+    wait_all([column_ref], send_sem, 0)
+
+
+def owner_call(kernel, out, scratch, collective_id, *operands):
+    vmem = pl.BlockSpec(memory_space=pltpu.VMEM)
+    return pl.pallas_call(
+        kernel,
+        out_shape=out,
+        in_specs=[vmem] * len(operands),
+        out_specs=vmem,
+        scratch_shapes=scratch
+        + [pltpu.SemaphoreType.DMA((2,)), pltpu.SemaphoreType.DMA((2,))],
+        compiler_params=pltpu.CompilerParams(collective_id=collective_id, has_side_effects=True),
+        name="owner" + str(collective_id),
+    )(*operands)
 
 
 def body(source_points, target_points, source_mass, target_mass, support, coarse_potential):
@@ -154,27 +274,32 @@
     named = flat_owner[None, :] == jnp.arange(devices, dtype=jnp.int32)[:, None]
     first = jnp.min(jnp.where(named, flat_within[None, :], local_count), axis=1)
     second = jnp.max(jnp.where(named, flat_within[None, :], -1), axis=1)
-    request = jnp.stack([first, second], axis=1)
+    request = jnp.stack([first, second], axis=1).astype(jnp.int32)
+    shape = (devices, CAP, points)
+    (asked,) = exchange([jnp.broadcast_to(request[:, :, None], shape)], 0)
     first_of = jnp.sum(jnp.where(named, first[:, None], 0), axis=0).reshape(owner.shape)
     slot_list = (owner * CAP + (within > first_of).astype(jnp.int32)).astype(jnp.int32)
-    asked = exchange(request)
 
     target_sq = squares(target_points)
     source_sq = squares(source_points)
     u = 2.0 * (coarse_potential - target_sq) + target_mass
-    tiles = exchange(target_points[asked]).reshape(devices * CAP, features, points)
-    flat_asked = asked.reshape(-1)
-    matches = flat_asked[:, None] == jnp.arange(local_count, dtype=jnp.int32)[None, :]
+    matches = asked[:, :, None, :] == jnp.arange(local_count, dtype=jnp.int32)[:, None]
+    sending = jnp.sum(jnp.where(matches, u, 0.0), axis=2)
+    tiles, received = exchange([target_points[asked[:, :, 0]], sending], 1)
+    tiles = tiles.reshape(devices * CAP, features, points)
+    row_shape = jax.ShapeDtypeStruct(shape, jnp.float32)
+    level_shape = jax.ShapeDtypeStruct(target_mass.shape, jnp.float32)
+    buffer = pltpu.VMEM(shape, jnp.float32)
     for sweep in range(ITERS):
-        sending = jnp.sum(jnp.where(matches[:, :, None], u[None, :, :], 0.0), axis=1)
-        received = exchange(sending.reshape(devices, CAP, points)).reshape(devices * CAP, points)
-        level, column = sweep_call(slot_list, source_points, source_mass, tiles, received)
-        peer = exchange(column.reshape(devices, CAP, points)).reshape(devices * CAP, points)
-        masked = jnp.where(matches[:, :, None], peer[:, None, :], lowest)
-        upper = jnp.max(masked, axis=0)
-        total = jnp.sum(jnp.exp(masked - upper[None]), axis=0)
-        column_level = upper + jnp.log(total)
-        u = target_mass - column_level
+        level, column = sweep_call(
+            slot_list, source_points, source_mass, tiles, received.reshape(devices * CAP, points)
+        )
+        column = column.reshape(shape)
+        if sweep < ITERS - 1:
+            received = owner_call(
+                turn_kernel, row_shape, [buffer, buffer], 2 + sweep, column, asked, target_mass
+            )
+    column_level = owner_call(finish_kernel, level_shape, [buffer], 1 + ITERS, column, asked)
     return (source_sq - 0.5 * level, target_sq - 0.5 * column_level)
 
 

time: 143 us -> 128 us (0.90)
  Pallas kernels: 49.3 us -> 118 us
  waiting for transfers between devices: 50.3 us -> 0 us
  starting transfers between devices: 17.8 us -> 0 us
  blocking collectives: 10.8 us -> 0 us
  other arithmetic: 7.19 us -> 4.63 us
  local copies, waits for them, and re-layouts: 6.21 us -> 4.74 us
    pallas_call x0 -> x4, Pallas kernels: none -> 68.2 us  [the longest x2 36 us: exchange(): pl.pallas_call(functools.partial(exchange_kernel, count), out_shape=tuple...]
    all_to_all x5 -> x0, waiting for transfers between devices: 50.3 us -> none  [exchange(): return lax.all_to_all(array, AXES, split_axis=0, concat_axis=0, tiled=True)]
    all_to_all x5 -> x0, starting transfers between devices: 17.8 us -> none  [exchange(): return lax.all_to_all(array, AXES, split_axis=0, concat_axis=0, tiled=True)]
    all_to_all x1 -> x0, blocking collectives: 10.8 us -> none  [exchange(): return lax.all_to_all(array, AXES, split_axis=0, concat_axis=0, tiled=True)]
  transfers between devices with their start and end apart: 5 -> 0, of which waited for: 5 -> 0; matrix products, arithmetic and copies ran while one was open for 3% -> 0% of each run, Pallas kernels for 0% -> 0%
where the time goes in v2:
time: 128 us
  Pallas kernels  118 us (92%)
  local copies, waits for them, and re-layouts  4.74 us (4%)
  other arithmetic  4.63 us (4%)
    pallas_call x2, Pallas kernels, sweep_call(): pl.pallas_call(sweep_kernel, out_shape=(jax.ShapeDtypeStruct((clusters, p...  49.4 us
    pallas_call x2, Pallas kernels, exchange(): pl.pallas_call(functools.partial(exchange_kernel, count), out_shape=tuple...  36 us
    pallas_call x2, Pallas kernels, owner_call(): pl.pallas_call(kernel, out_shape=out, in_specs=[vmem] * len(operands), ou...  32.1 us

profile of v2, /device:TPU:0, one launch (start us, length us, event | category | flops | bytes accessed | tf_op | source)
XLA Modules:
  0.0 127.7 jit_solution(672732287857608224)
XLA Ops:
  0.6 0.7 add_select_fusion.1
  1.3 0.1 eq.30
  1.4 0.1 broadcast_in_dim.52
  1.5 0.1 select_reduce_fusion.1
  1.6 0.1 copy.10
  1.7 0.7 broadcast_in_dim.59.refs_0_
  2.4 10.8 %exchange0.1.asked_ref = s32[32,2,128]{2,1,0:T(2,128)} custom-call(s32[32,2,128]{2,1,0:T(2,128)} %broadcast_in_dim.59.refs_0_), custom_call_target="tpu_custom_call" | custom-call | tf_op jit(solution)/shard_map/exchange0/pallas_call | solution.py:210
  13.3 1.0 multiply_reduce_fusion
  14.3 0.7 copy-done.1
  15.1 0.7 select_reduce_fusion.refs_1_
  15.8 0.6 fusion
  16.4 0.1 reshape.35
  16.6 1.7 %gather_fusion = bf16[64,64,128]{2,1,0:T(8,128)(2,1)} fusion(bf16[16,64,128]{2,1,0:T(8,128)(2,1)S(1)} %copy-done, s32[1024]{0:T(1024)S(1)} %pad_clamp_fusion), kind=kCustom, calls=%fused_computation | custom fusion | bytes 2097408 | tf_op jit(solution)/shard_map/gather | solution.py:288
  18.3 25.2 %exchange1.1 = (bf16[32,2,64,128]{3,2,1,0:T(8,128)(2,1)}, f32[32,2,128]{2,1,0:T(2,128)}) custom-call(bf16[32,2,64,128]{3,2,1,0:T(8,128)(2,1)} %bitcast.8, f32[32,2,128]{2,1,0:T(2,128)} %select_reduce_fusion.refs_1_), custom_call_target="tpu_custom_call" | custom-call | tf_op jit(solution)/shard_map/exchange1/pallas_call | solution.py:210
  43.5 0.1 select_reduce_fusion.2
  43.6 0.1 reshape.27
  43.7 0.5 copy-done.3
  44.2 0.6 convert_add_fusion.slots_ref
  44.8 24.7 %sweep.2 = (f32[16,128]{1,0:T(8,128)}, f32[64,128]{1,0:T(8,128)}) custom-call(s32[16,32]{1,0:T(8,128)} %convert_add_fusion.slots_ref, bf16[16,64,128]{2,1,0:T(8,128)(2,1)} %source_ref.3, f32[16,128]{1,0:T(8,128)} %mass_ref.5, bf16[64,64,128]{2,1,0:T(8,128)(2,1)} %bitcast.14, f32[64,128]{1,0:T(8,128)} %bitcast.16), custom_call_target="tpu_custom_call" | custom-call | flops 4294967296 | bytes 1048576 | tf_op jit(solution)/shard_map/sweep/pallas_call | solution.py:124
  69.5 22.4 %owner2.1 = f32[32,2,128]{2,1,0:T(2,128)} custom-call(f32[32,2,128]{2,1,0:T(2,128)} %bitcast.11, s32[32,2,128]{2,1,0:T(2,128)} %exchange0.1.asked_ref, f32[16,128]{1,0:T(8,128)} %mass_ref.4), custom_call_target="tpu_custom_call" | custom-call | tf_op jit(solution)/shard_map/owner2/pallas_call | solution.py:256
  91.9 24.7 %sweep.3 = (f32[16,128]{1,0:T(8,128)}, f32[64,128]{1,0:T(8,128)}) custom-call(s32[16,32]{1,0:T(8,128)} %convert_add_fusion.slots_ref, bf16[16,64,128]{2,1,0:T(8,128)(2,1)} %source_ref.3, f32[16,128]{1,0:T(8,128)} %mass_ref.5, bf16[64,64,128]{2,1,0:T(8,128)(2,1)} %bitcast.15, f32[64,128]{1,0:T(8,128)} %bitcast.10), custom_call_target="tpu_custom_call" | custom-call | flops 4294967296 | bytes 1048576 | tf_op jit(solution)/shard_map/sweep/pallas_call | solution.py:124
  116.6 9.7 %owner3.1 = f32[16,128]{1,0:T(8,128)} custom-call(f32[32,2,128]{2,1,0:T(2,128)} %bitcast.9, s32[32,2,128]{2,1,0:T(2,128)} %exchange0.1.asked_ref), custom_call_target="tpu_custom_call" | custom-call | tf_op jit(solution)/shard_map/owner3/pallas_call | solution.py:256
  126.5 0.6 copy-done.4
  127.1 0.6 multiply_subtract_fusion
  (17 shorter events, 0.1 us)
Async XLA Ops:
  2.4 14.1 %copy-start = (bf16[16,64,128]{2,1,0:T(8,128)(2,1)S(1)}, bf16[16,64,128]{2,1,0:T(8,128)(2,1)}, u32[]{:S(2)}) copy-start(bf16[16,64,128]{2,1,0:T(8,128)(2,1)} %param.7) | copy-start | bytes 786436
  13.2 1.1 copy-start.5
  13.3 1.1 copy-start.6
  14.3 0.8 copy-start.1
  43.5 0.7 copy-start.3
  91.9 34.5 %copy-start.2 = (bf16[16,64,128]{2,1,0:T(8,128)(2,1)S(1)}, bf16[16,64,128]{2,1,0:T(8,128)(2,1)}, u32[]{:S(2)}) copy-start(bf16[16,64,128]{2,1,0:T(8,128)(2,1)} %source_ref.3) | copy-start | bytes 786436
  126.4 0.7 copy-start.4
  126.4 0.7 copy-start.7
